TPU v7x, 256 devices: a whole 4x4x8 slice. The times are simulated.
256 devices in a mesh: state: 256 (over y, z, x, core).
Axes of the slice: x: 4, y: 4, z: 8, core: 2. Of those that a mesh axis runs over, the one named last changes fastest.
Arguments:
- transitions: float32 [4096, 16, 4096], P('state'), may hold values from 0 to 1, as said below
- costs: float32 [4096, 16, 128], P('state'), may hold values from 0 to 4
- valid_counts: int32 [4096], P('state'), may hold values from 1 to 16
- start_values: float32 [4096, 128], P('state'), may hold values from -12 to 12
- ref_state: int32 [1], replicated, may hold values from 0 to 4095
Outputs:
- relative_values: float32 [4096, 128], P('state')
- lower_bounds: float32 [4, 128], replicated
- upper_bounds: float32 [4, 128], replicated
Inputs may be any that keep to these rules, and one draw needn't show every extreme that they name: Every entry is nonnegative and each row transitions[s, a, :] sums to one up to float32 rounding. Actions 0 to valid_counts[s] - 1 are allowed in state s.
All inputs are finite; a program needn't handle non-finite values.
Results may differ from a plain program's by a relative error of at most 0.00017.
Values sent between devices are 32-bit elements; how exact they have to be, the bound alone decides.
No kernel may reach another device: no remote copies, remote signals or barrier semaphores. Data moves between devices by JAX's collectives and lax.ppermute only.
A program may use at most 64 MiB of HBM per device.

v0:
```python
import jax
import jax.numpy as jnp
from jax import lax
from jax.sharding import Mesh
from jax.sharding import PartitionSpec as P

ITERS = 4
STATE = ("state_0", "state_1", "state_2", "state_3")
big_value = 1e30


def over_axes(x, axes):
    for axis in axes:
        x = lax.pmax(x, axis)
    return x


def local(transitions, costs, valid_counts, start_values, ref_state):
    local_states = transitions.shape[0]
    actions = transitions.shape[1]
    scenarios = start_values.shape[1]
    flat_rows = transitions.reshape(local_states * actions, transitions.shape[2])
    allowed = jnp.arange(actions, dtype=jnp.int32)[None, :] < valid_counts[:, None]
    my_index = lax.axis_index(STATE)
    first_state = my_index * local_states
    owner_index = ref_state[0] // local_states
    offset = jnp.clip(ref_state[0] - first_state, 0, local_states - 1)
    is_owner = owner_index == my_index
    lower_list = []
    upper_list = []
    unshifted = start_values
    for iteration in range(ITERS):
        field_all = lax.all_gather(unshifted, STATE, axis=0, tiled=True)
        bellman_expected = jnp.dot(
            flat_rows,
            field_all,
            precision=lax.Precision.HIGHEST,
            preferred_element_type=jnp.float32,
        )
        q_values = costs + bellman_expected.reshape(local_states, actions, scenarios)
        q_values = jnp.where(allowed[:, :, None], q_values, jnp.float32(big_value))
        best_value = jnp.min(q_values, axis=1)
        increase = best_value - unshifted
        lower_list.append(jnp.min(increase, axis=0))
        upper_list.append(jnp.max(increase, axis=0))
        unshifted = best_value
    local_row = lax.dynamic_slice_in_dim(unshifted, offset, 1, 0)
    masked_row = jnp.where(is_owner, local_row, jnp.float32(-big_value))
    ref_row, upper_all, negated_all = (
        over_axes(masked_row, STATE),
        over_axes(jnp.stack(upper_list), STATE),
        over_axes(-jnp.stack(lower_list), STATE),
    )
    return (unshifted - ref_row, -negated_all, upper_all)


def solution(mesh):
    split = Mesh(mesh.devices.reshape(4, 8, 4, 2), ("state_0", "state_1", "state_2", "state_3"))
    return jax.shard_map(
        local,
        mesh=split,
        in_specs=(P(STATE, None, None), P(STATE, None, None), P(STATE), P(STATE, None), P()),
        out_specs=(P(STATE, None), P(), P()),
        check_vma=False,
    )
```

profile of v0, /device:TPU:1, one launch (start us, length us, event | category | flops | bytes accessed | tf_op | source)
XLA Modules:
  0.0 506.4 jit_solution(16758565774394789343)
XLA Ops:
  7.2 0.0 all-gather.5.cloned.1.call-start
  7.2 0.7 all-gather.5.cloned.1.call-update
  7.9 0.0 all-gather.7.cloned.1.call-start
  7.9 0.7 iota_compare_fusion
  8.7 111.4 %all-gather.5.cloned.1.call-done = f32[4096,128]{1,0:T(8,128)} async-done(((f32[16,128]{1,0:T(8,128)}), f32[4096,128]{1,0:T(8,128)}) %all-gather.5.cloned.1.call-update) | async-done | bytes 2097168 | tf_op jit(solution)/shard_map/all_gather | solution.py:33
  120.0 6.9 %fusion.8 = f32[16,128]{1,0:T(8,128)} fusion(f32[16,16,128]{2,1,0:T(8,128)} %param.6, f32[16,16,4096]{2,1,0:T(8,128)} %param.5, f32[4096,128]{1,0:T(8,128)} %all-gather.5.cloned.1.call-done, pred[16,16]{1,0:T(8,128)(4,1)S(1)} %iota_compare_fusion), kind=kOutput, calls=%fused_computation.7 | convolution fusion | flops 1610708992 | bytes 6430976 | tf_op jit(solution)/shard_map/dot_general | solution.py:34
  127.0 0.0 all-gather.7.cloned.1.call-update
  127.0 0.0 all-gather.9.cloned.1.call-start
  127.1 103.3 %all-gather.7.cloned.1.call-done = f32[4096,128]{1,0:T(8,128)} async-done(((f32[16,128]{1,0:T(8,128)}), f32[4096,128]{1,0:T(8,128)}) %all-gather.7.cloned.1.call-update) | async-done | bytes 2097168 | tf_op jit(solution)/shard_map/all_gather | solution.py:33
  230.3 6.3 %convolution_bitcast_fusion.2 = f32[256,128]{0,1:T(8,128)S(1)} fusion(f32[4096,128]{1,0:T(8,128)} %all-gather.7.cloned.1.call-done, f32[256,4096]{1,0:T(8,128)} %bitcast.44), kind=kOutput, calls=%fused_computation.6 | convolution fusion | flops 1610612736 | bytes 6422528 | tf_op jit(solution)/shard_map/dot_general | solution.py:34
  236.6 0.1 copy.8
  236.7 0.0 copy-done
  236.8 0.7 select_reduce_fusion.2
  237.5 0.0 all-gather.9.cloned.1.call-update
  237.5 0.2 all-gather.11.cloned.1.call-start
  237.7 103.1 %all-gather.9.cloned.1.call-done = f32[4096,128]{1,0:T(8,128)} async-done(((f32[16,128]{1,0:T(8,128)}), f32[4096,128]{1,0:T(8,128)}) %all-gather.9.cloned.1.call-update) | async-done | bytes 2097168 | tf_op jit(solution)/shard_map/all_gather | solution.py:33
  340.8 6.3 %convolution_bitcast_fusion.1 = f32[256,128]{0,1:T(8,128)S(1)} fusion(f32[4096,128]{1,0:T(8,128)} %all-gather.9.cloned.1.call-done, f32[256,4096]{1,0:T(8,128)} %bitcast.45), kind=kOutput, calls=%fused_computation.5 | convolution fusion | flops 1610612736 | bytes 6422528 | tf_op jit(solution)/shard_map/dot_general | solution.py:34
  347.1 0.1 copy.9
  347.2 0.7 select_reduce_fusion.1
  347.9 0.0 all-gather.11.cloned.1.call-update
  348.6 0.0 copy-start.1
  348.6 0.0 copy-start.4
  348.6 102.6 %all-gather.11.cloned.1.call-done = f32[4096,128]{1,0:T(8,128)} async-done(((f32[16,128]{1,0:T(8,128)}), f32[4096,128]{1,0:T(8,128)}) %all-gather.11.cloned.1.call-update) | async-done | bytes 2097168 | tf_op jit(solution)/shard_map/all_gather | solution.py:33
  451.2 6.3 %convolution_bitcast_fusion = f32[256,128]{0,1:T(8,128)S(1)} fusion(f32[4096,128]{1,0:T(8,128)} %all-gather.11.cloned.1.call-done, f32[256,4096]{1,0:T(8,128)} %bitcast.46), kind=kOutput, calls=%fused_computation.4 | convolution fusion | flops 1610612736 | bytes 6422528 | tf_op jit(solution)/shard_map/dot_general | solution.py:34
  457.5 0.1 copy.10
  457.6 0.1 select_reduce_fusion
  457.8 8.5 %all-reduce.2 = (f32[1,128]{1,0:T(1,128)S(1)}, f32[4,128]{1,0:T(4,128)S(1)}, f32[4,128]{1,0:T(4,128)S(1)}) all-reduce(f32[1,128]{1,0:T(1,128)S(1)} %broadcast_select_fusion, f32[4,128]{1,0:T(4,128)S(1)} %get-tuple-element.29, ...), channel_id=1, replica_groups=mesh['state_0'=4,'state_1'=8,'state_2'=4,'state_3'=2] {'state_0'}, use_global_device_ids=true, to_apply=%region_4.5 | all-reduce | flops 1152 | bytes 9216 | tf_op jit(solution)/shard_map/pmax | solution.py:14
  466.4 13.0 %all-reduce = (f32[1,128]{1,0:T(1,128)S(1)}, f32[4,128]{1,0:T(4,128)S(1)}, f32[4,128]{1,0:T(4,128)S(1)}) all-reduce(f32[1,128]{1,0:T(1,128)S(1)} %get-tuple-element.23, f32[4,128]{1,0:T(4,128)S(1)} %get-tuple-element.24, f32[4,128]{1,0:T(4,128)S(1)} %get-tuple-element.25), channel_id=1, replica_groups=mesh['state_0'=4,'state_1'=8,'state_2'=4,'state_3'=2] {'state_1'}, use_global_device_ids=true, to_apply=%region_5.6 | all-reduce | flops 1152 | bytes 9216 | tf_op jit(solution)/shard_map/pmax | solution.py:14
  479.4 8.5 %all-reduce.1 = (f32[1,128]{1,0:T(1,128)S(1)}, f32[4,128]{1,0:T(4,128)S(1)}, f32[4,128]{1,0:T(4,128)S(1)}) all-reduce(f32[1,128]{1,0:T(1,128)S(1)} %get-tuple-element.17, f32[4,128]{1,0:T(4,128)S(1)} %get-tuple-element.18, f32[4,128]{1,0:T(4,128)S(1)} %get-tuple-element.19), channel_id=1, replica_groups=mesh['state_0'=4,'state_1'=8,'state_2'=4,'state_3'=2] {'state_2'}, use_global_device_ids=true, to_apply=%region_6.7 | all-reduce | flops 1152 | bytes 9216 | tf_op jit(solution)/shard_map/pmax | solution.py:14
  487.9 10.8 %all-reduce.3 = (f32[128]{0:T(128)S(1)}, f32[4,128]{1,0:T(4,128)S(1)}, f32[4,128]{1,0:T(4,128)}) all-reduce(f32[128]{0:T(128)S(1)} %bitcast.55, f32[4,128]{1,0:T(4,128)S(1)} %get-tuple-element.21, f32[4,128]{1,0:T(4,128)S(1)} %get-tuple-element.22), channel_id=1, replica_groups=mesh['state_0'=4,'state_1'=8,'state_2'=4,'state_3'=2] {'state_3'}, use_global_device_ids=true, to_apply=%region_7.8 | all-reduce | flops 1152 | bytes 9216 | tf_op jit(solution)/shard_map/pmax | solution.py:14
  498.7 0.6 broadcast_subtract_fusion
  499.3 0.6 neg.7
  (10 shorter events, 0.1 us)
Async XLA Ops:
  7.2 112.9 %all-gather.5.cloned.1.call-start = ((), (), s32[]{:S(2)}) async-start(), calls=%async_computation | async-start | bytes 2105344 | tf_op jit(solution)/shard_map/all_gather | solution.py:33
  7.9 222.4 %all-gather.7.cloned.1.call-start = ((), (), s32[]{:S(2)}) async-start(), calls=%async_computation.1 | async-start | bytes 2105344 | tf_op jit(solution)/shard_map/all_gather | solution.py:33
  127.0 213.8 %all-gather.9.cloned.1.call-start = ((), (), s32[]{:S(2)}) async-start(), calls=%async_computation.2 | async-start | bytes 2105344 | tf_op jit(solution)/shard_map/all_gather | solution.py:33
  230.3 6.4 %copy-start = (f32[16,16,128]{2,1,0:T(8,128)S(1)}, f32[16,16,128]{2,1,0:T(8,128)}, u32[]{:S(2)}) copy-start(f32[16,16,128]{2,1,0:T(8,128)} %param.6) | copy-start | bytes 393220
  237.5 213.7 %all-gather.11.cloned.1.call-start = ((), (), s32[]{:S(2)}) async-start(), calls=%async_computation.3 | async-start | bytes 2105344 | tf_op jit(solution)/shard_map/all_gather | solution.py:33
  348.6 109.1 %copy-start.1 = (f32[16,128]{1,0:T(8,128)S(1)}, f32[16,128]{1,0:T(8,128)}, u32[]{:S(2)}) copy-start(f32[16,128]{1,0:T(8,128)} %fusion.8) | copy-start | bytes 24580
  348.6 109.1 %copy-start.2 = (f32[16,128]{1,0:T(8,128)S(1)}, f32[16,128]{1,0:T(8,128)}, u32[]{:S(2)}) copy-start(f32[16,128]{1,0:T(8,128)} %select_reduce_fusion.2) | copy-start | bytes 24580
  348.6 109.1 %copy-start.3 = (f32[16,128]{1,0:T(8,128)S(1)}, f32[16,128]{1,0:T(8,128)}, u32[]{:S(2)}) copy-start(f32[16,128]{1,0:T(8,128)} %select_reduce_fusion.1) | copy-start | bytes 24580
  348.6 109.1 %copy-start.4 = (f32[16,128]{1,0:T(8,128)S(1)}, f32[16,128]{1,0:T(8,128)}, u32[]{:S(2)}) copy-start(f32[16,128]{1,0:T(8,128)} %param.8) | copy-start | bytes 24580
Sparse Core Ops, SparseCore 0:
  11.7 108.2 all-gather.4
  127.1 103.1 all-gather.6
  237.6 103.1 all-gather.8
  348.0 103.1 all-gather.10
where the time goes:
time: 507 us; the launch traced here: 506 us
  waiting for transfers between devices  421 us (83%)
  blocking collectives  40.9 us (8%)
  matrix products  25.8 us (5%)
  between operations  14.6 us (3%)
    all_gather x4, waiting for transfers between devices, local(): field_all = lax.all_gather(unshifted, STATE, axis=0, tiled=True)  420 us
    pmax x4, blocking collectives, over_axes(): x = lax.pmax(x, axis)  40.9 us
    dot_general x4, matrix products, local(): jnp.dot(flat_rows, field_all, precision=lax.Precision.HIGHEST, preferred_...  25.8 us
  transfers between devices with their start and end apart: 4, of which 4 were waited for; matrix products, arithmetic and copies ran while one was open for 0% of the time, Pallas kernels for 0%

commit v1 on v0

--- a/solution.py
+++ b/solution.py
@@ -30,7 +30,8 @@
     upper_list = []
     unshifted = start_values
     for iteration in range(ITERS):
-        field_all = lax.all_gather(unshifted, STATE, axis=0, tiled=True)
+        sent = jnp.stack([unshifted] * lax.axis_size(STATE))
+        field_all = jnp.concatenate(lax.all_to_all(sent, STATE, 0, 0), axis=0)
         bellman_expected = jnp.dot(
             flat_rows,
             field_all,

time: 507 us -> 310 us (0.61)
  waiting for transfers between devices: 421 us -> 106 us
  blocking collectives: 40.9 us -> 156 us
  starting transfers between devices: 0.34 us -> 22.1 us
  between operations: 14.6 us -> 1.5 us
  matrix products: 25.8 us -> 18.5 us
    all_gather x4 -> x0, waiting for transfers between devices: 420 us -> none  [local(): field_all = lax.all_gather(unshifted, STATE, axis=0, tiled=True)]
    all_to_all x0 -> x2, blocking collectives: none -> 119 us  [local(): field_all = jnp.concatenate(lax.all_to_all(sent, STATE, 0, 0), axis=0)]
    all_to_all x0 -> x2, waiting for transfers between devices: none -> 106 us  [local(): field_all = jnp.concatenate(lax.all_to_all(sent, STATE, 0, 0), axis=0)]
    all_to_all x0 -> x2, starting transfers between devices: none -> 22.1 us  [local(): field_all = jnp.concatenate(lax.all_to_all(sent, STATE, 0, 0), axis=0)]
    dot_general x4, matrix products: 25.8 us -> 18.5 us  [local(): jnp.dot(flat_rows, field_all, precision=lax.Precision.HIGHEST, preferred_...]
  transfers between devices with their start and end apart: 4 -> 2, of which waited for: 4 -> 2; matrix products, arithmetic and copies ran while one was open for 0% -> 0% of each run, Pallas kernels for 0% -> 0%
where the time goes in v1:
time: 310 us
  blocking collectives  156 us (50%)
  waiting for transfers between devices  106 us (34%)
  starting transfers between devices  22.1 us (7%)
  matrix products  18.5 us (6%)
  local copies, waits for them, and re-layouts  4.23 us (1%)
    all_to_all x2, blocking collectives, local(): field_all = jnp.concatenate(lax.all_to_all(sent, STATE, 0, 0), axis=0)  119 us
    all_to_all x2, waiting for transfers between devices, local(): field_all = jnp.concatenate(lax.all_to_all(sent, STATE, 0, 0), axis=0)  106 us
    pmax x4, blocking collectives, over_axes(): x = lax.pmax(x, axis)  36.8 us
    all_to_all x2, starting transfers between devices, local(): field_all = jnp.concatenate(lax.all_to_all(sent, STATE, 0, 0), axis=0)  22.1 us
    dot_general x4, matrix products, local(): jnp.dot(flat_rows, field_all, precision=lax.Precision.HIGHEST, preferred_...  18.5 us
  transfers between devices with their start and end apart: 2, of which 2 were waited for; matrix products, arithmetic and copies ran while one was open for 0% of the time, Pallas kernels for 0%

profile of v1, /device:TPU:1, one launch (start us, length us, event | category | flops | bytes accessed | tf_op | source)
XLA Modules:
  0.0 309.7 jit_solution(7165057655994753762)
XLA Ops:
  0.6 2.2 stack.28
  2.8 15.6 %all-to-all-start = ((f32[256,16,128]{2,1,0:T(8,128)}), f32[256,16,128]{2,1,0:T(8,128)S(1)}, u32[]{:S(2)}, u32[]{:S(2)}) async-start(f32[256,16,128]{2,1,0:T(8,128)} %stack.28), calls=%async_computation | async-start | bytes 4194304 | tf_op jit(solution)/shard_map/all_to_all | solution.py:34
  18.5 0.0 copy-done.4
  18.5 0.1 iota_compare_fusion
  18.6 53.2 %all-to-all-done = f32[256,16,128]{2,1,0:T(8,128)S(1)} async-done(((f32[256,16,128]{2,1,0:T(8,128)}), f32[256,16,128]{2,1,0:T(8,128)S(1)}, u32[]{:S(2)}, u32[]{:S(2)}) %all-to-all-start) | async-done | bytes 2097184 | tf_op jit(solution)/shard_map/all_to_all | solution.py:34
  71.8 0.0 copy-done.2
  71.8 5.7 %fusion.1 = f32[16,128]{1,0:T(8,128)S(1)} fusion(f32[16,16,128]{2,1,0:T(8,128)S(1)} %copy-done.2, f32[16,16,4096]{2,1,0:T(8,128)} %param.5, f32[4096,128,1]{1,0,2:T(8,128)S(1)} %bitcast.46, pred[16,16]{1,0:T(8,128)(4,1)S(1)} %iota_compare_fusion), kind=kOutput, calls=%fused_computation.5 | convolution fusion | flops 1610708992 | bytes 6430976 | tf_op jit(solution)/shard_map/dot_general | solution.py:35
  77.5 0.1 stack.29
  77.7 0.0 copy-start
  77.7 59.5 %all_to_all.20 = f32[256,16,128]{2,1,0:T(8,128)S(1)} all-to-all(f32[256,16,128]{2,1,0:T(8,128)S(1)} %stack.29), channel_id=1, replica_groups=mesh['state_0'=4,'state_1'=8,'state_2'=4,'state_3'=2] {'state_0','state_..., dimensions={0} | all-to-all | bytes 4194304 | tf_op jit(solution)/shard_map/all_to_all | solution.py:34
  137.2 0.0 copy-done
  137.2 3.6 %convolution_bitcast_fusion.2 = f32[256,128]{0,1:T(8,128)S(1)} fusion(f32[4096,128]{1,0:T(8,128)S(1)} %bitcast.47, f32[256,4096]{1,0:T(8,128)S(1)} %bitcast.43), kind=kOutput, calls=%fused_computation.2 | convolution fusion | flops 1610612736 | bytes 6422528 | tf_op jit(solution)/shard_map/dot_general | solution.py:35
  140.8 0.1 copy.8
  140.9 0.1 select_reduce_fusion.2
  141.0 0.1 stack.30
  141.2 0.0 copy-start.1
  141.2 59.5 %all_to_all.21 = f32[256,16,128]{2,1,0:T(8,128)S(1)} all-to-all(f32[256,16,128]{2,1,0:T(8,128)S(1)} %stack.30), channel_id=1, replica_groups=mesh['state_0'=4,'state_1'=8,'state_2'=4,'state_3'=2] {'state_0','state_..., dimensions={0} | all-to-all | bytes 4194304 | tf_op jit(solution)/shard_map/all_to_all | solution.py:34
  200.7 3.6 %convolution_bitcast_fusion.1 = f32[256,128]{0,1:T(8,128)S(1)} fusion(f32[4096,128]{1,0:T(8,128)S(1)} %bitcast.48, f32[256,4096]{1,0:T(8,128)S(1)} %bitcast.44), kind=kOutput, calls=%fused_computation.1 | convolution fusion | flops 1610612736 | bytes 6422528 | tf_op jit(solution)/shard_map/dot_general | solution.py:35
  204.3 0.1 copy.9
  204.4 0.1 select_reduce_fusion.1
  204.5 1.5 stack.31
  206.0 6.4 %all-to-all-start.3 = ((f32[256,16,128]{2,1,0:T(8,128)}), f32[256,16,128]{2,1,0:T(8,128)S(1)}, u32[]{:S(2)}, u32[]{:S(2)}) async-start(f32[256,16,128]{2,1,0:T(8,128)} %stack.31), calls=%async_computation.3 | async-start | bytes 4194304 | tf_op jit(solution)/shard_map/all_to_all | solution.py:34
  213.1 52.6 %all-to-all-done.3 = f32[256,16,128]{2,1,0:T(8,128)S(1)} async-done(((f32[256,16,128]{2,1,0:T(8,128)}), f32[256,16,128]{2,1,0:T(8,128)S(1)}, u32[]{:S(2)}, u32[]{:S(2)}) %all-to-all-start.3) | async-done | bytes 2097184 | tf_op jit(solution)/shard_map/all_to_all | solution.py:34
  265.8 5.7 %convolution_bitcast_fusion = f32[256,128]{0,1:T(8,128)S(1)} fusion(f32[4096,128]{1,0:T(8,128)S(1)} %bitcast.45, f32[256,4096]{1,0:T(8,128)} %bitcast.42), kind=kOutput, calls=%fused_computation | convolution fusion | flops 1610612736 | bytes 6422528 | tf_op jit(solution)/shard_map/dot_general | solution.py:35
  271.4 0.1 copy.10
  271.5 0.1 select_reduce_fusion
  271.7 6.8 %all-reduce.2 = (f32[1,128]{1,0:T(1,128)S(1)}, f32[4,128]{1,0:T(4,128)S(1)}, f32[4,128]{1,0:T(4,128)S(1)}) all-reduce(f32[1,128]{1,0:T(1,128)S(1)} %broadcast_select_fusion, f32[4,128]{1,0:T(4,128)S(1)} %get-tuple-element.29, ...), channel_id=1, replica_groups=mesh['state_0'=4,'state_1'=8,'state_2'=4,'state_3'=2] {'state_0'}, use_global_device_ids=true, to_apply=%region_4.5 | all-reduce | flops 1152 | bytes 9216 | tf_op jit(solution)/shard_map/pmax | solution.py:14
  278.6 11.4 %all-reduce = (f32[1,128]{1,0:T(1,128)S(1)}, f32[4,128]{1,0:T(4,128)S(1)}, f32[4,128]{1,0:T(4,128)S(1)}) all-reduce(f32[1,128]{1,0:T(1,128)S(1)} %get-tuple-element.23, f32[4,128]{1,0:T(4,128)S(1)} %get-tuple-element.24, f32[4,128]{1,0:T(4,128)S(1)} %get-tuple-element.25), channel_id=1, replica_groups=mesh['state_0'=4,'state_1'=8,'state_2'=4,'state_3'=2] {'state_1'}, use_global_device_ids=true, to_apply=%region_5.6 | all-reduce | flops 1152 | bytes 9216 | tf_op jit(solution)/shard_map/pmax | solution.py:14
  289.9 7.4 %all-reduce.1 = (f32[1,128]{1,0:T(1,128)S(1)}, f32[4,128]{1,0:T(4,128)S(1)}, f32[4,128]{1,0:T(4,128)S(1)}) all-reduce(f32[1,128]{1,0:T(1,128)S(1)} %get-tuple-element.17, f32[4,128]{1,0:T(4,128)S(1)} %get-tuple-element.18, f32[4,128]{1,0:T(4,128)S(1)} %get-tuple-element.19), channel_id=1, replica_groups=mesh['state_0'=4,'state_1'=8,'state_2'=4,'state_3'=2] {'state_2'}, use_global_device_ids=true, to_apply=%region_6.7 | all-reduce | flops 1152 | bytes 9216 | tf_op jit(solution)/shard_map/pmax | solution.py:14
  297.4 11.1 %all-reduce.3 = (f32[128]{0:T(128)S(1)}, f32[4,128]{1,0:T(4,128)S(1)}, f32[4,128]{1,0:T(4,128)}) all-reduce(f32[128]{0:T(128)S(1)} %bitcast.57, f32[4,128]{1,0:T(4,128)S(1)} %get-tuple-element.21, f32[4,128]{1,0:T(4,128)S(1)} %get-tuple-element.22), channel_id=1, replica_groups=mesh['state_0'=4,'state_1'=8,'state_2'=4,'state_3'=2] {'state_3'}, use_global_device_ids=true, to_apply=%region_7.8 | all-reduce | flops 1152 | bytes 9216 | tf_op jit(solution)/shard_map/pmax | solution.py:14
  308.5 0.6 broadcast_subtract_fusion
  309.1 0.6 neg.7
  (8 shorter events, 0.1 us)
Async XLA Ops:
  2.8 15.7 %copy-start.4 = (s32[16]{0:T(128)S(1)}, s32[16]{0:T(128)}, u32[]{:S(2)}) copy-start(s32[16]{0:T(128)} %param.7) | copy-start | bytes 196
  2.8 69.0 %copy-start.2 = (f32[16,16,128]{2,1,0:T(8,128)S(1)}, f32[16,16,128]{2,1,0:T(8,128)}, u32[]{:S(2)}) copy-start(f32[16,16,128]{2,1,0:T(8,128)} %param.6) | copy-start | bytes 393220
  2.8 69.0 %all-to-all-start = ((f32[256,16,128]{2,1,0:T(8,128)}), f32[256,16,128]{2,1,0:T(8,128)S(1)}, u32[]{:S(2)}, u32[]{:S(2)}) async-start(f32[256,16,128]{2,1,0:T(8,128)} %stack.28), calls=%async_computation | async-start | bytes 4194304 | tf_op jit(solution)/shard_map/all_to_all | solution.py:34
  77.7 59.6 %copy-start = (f32[16,16,4096]{2,1,0:T(8,128)S(1)}, f32[16,16,4096]{2,1,0:T(8,128)}, u32[]{:S(2)}) copy-start(f32[16,16,4096]{2,1,0:T(8,128)} %param.5) | copy-start | bytes 12582916
  141.2 59.6 %copy-start.1 = (f32[16,16,4096]{2,1,0:T(8,128)S(1)}, f32[16,16,4096]{2,1,0:T(8,128)}, u32[]{:S(2)}) copy-start(f32[16,16,4096]{2,1,0:T(8,128)} %param.5) | copy-start | bytes 12582916
  206.0 59.7 %all-to-all-start.3 = ((f32[256,16,128]{2,1,0:T(8,128)}), f32[256,16,128]{2,1,0:T(8,128)S(1)}, u32[]{:S(2)}, u32[]{:S(2)}) async-start(f32[256,16,128]{2,1,0:T(8,128)} %stack.31), calls=%async_computation.3 | async-start | bytes 4194304 | tf_op jit(solution)/shard_map/all_to_all | solution.py:34
  265.8 5.9 %copy-start.3 = (f32[16,128]{1,0:T(8,128)S(1)}, f32[16,128]{1,0:T(8,128)}, u32[]{:S(2)}) copy-start(f32[16,128]{1,0:T(8,128)} %param.8) | copy-start | bytes 24580
